TPU v7x, 128 devices: a whole 4x4x4 slice. The times are simulated.
128 devices in a mesh: dp: 64 (over x, y, z), mp: 2 (over core).
Axes of the slice: x: 4, y: 4, z: 4, core: 2. Of those that a mesh axis runs over, the one named last changes fastest.
Arguments:
- view_one: bfloat16 [32768, 1024], P('dp'), may hold values from -40 to 40
- view_two: bfloat16 [32768, 1024], P('dp'), may hold values from -40 to 40
Outputs:
- gradient_one: bfloat16 [32768, 1024], P(('dp', 'mp'))
- gradient_two: bfloat16 [32768, 1024], P(('dp', 'mp'))
- loss_value: float32 [], replicated
All inputs are finite; a program needn't handle non-finite values.
Results may differ from a plain program's by a relative error of at most 0.013.
The roundings to bfloat16 on the way count: a program that leaves them out, or rounds other values in their place, can miss the bound.
Values may be sent and summed in bfloat16 or wider, within the bound.
A program may use at most 64 MiB of HBM per device.

v0:
```python
import jax
import jax.numpy as jnp
from jax import lax
from jax.sharding import PartitionSpec as P

ITERS = 3


epsilon = 1e-06


def copy_for_each(x, axis):
    length = lax.axis_size(axis)
    return lax.all_to_all(jnp.broadcast_to(x[None], (length, *x.shape)), axis, 0, 0, tiled=True)


def taken_together(x, axis):
    return copy_for_each(x, axis).sum(axis=0)


def packed_total(arrays, axis):
    ends = [0]
    for a in arrays:
        ends.append(ends[-1] + a.size)
    running = taken_together(jnp.concatenate([a.ravel() for a in arrays]), axis)
    return tuple((running[b:e].reshape(a.shape) for a, b, e in zip(arrays, ends, ends[1:])))


def gathered_total(x, axis):
    return lax.all_gather(x, axis).max(0)


def in_order(parts, dim):
    parts = jnp.moveaxis(parts, 0, dim)
    dims = parts.shape
    return parts.reshape(*dims[:dim], dims[dim] * dims[dim + 1], *dims[dim + 2 :])


def collect(x, axis, dim):
    parts = copy_for_each(x, axis)
    return in_order(parts, dim)


def side_by_side(arrays, axis, dim, along):
    ends, at = ([], 0)
    for a in arrays[:-1]:
        at += a.shape[along]
        ends.append(at)
    both = jnp.concatenate(arrays, axis=along)
    return tuple(jnp.split(lax.all_gather(both, axis, axis=dim, tiled=True), ends, axis=along))


def over_pieces(x, axis):
    parts = lax.all_gather(x, axis)
    return parts.sum(axis=0)


def schulz_step(full, normed_half, identity_half):
    product = jnp.dot(full, normed_half, preferred_element_type=jnp.float32).astype(jnp.bfloat16)
    target = (
        1.5 * identity_half - 0.5 * jnp.dot(full, product, preferred_element_type=jnp.float32)
    ).astype(jnp.bfloat16)
    return jnp.dot(full, target, preferred_element_type=jnp.float32)


def column_peak(matrix):
    return jnp.max(jnp.sum(jnp.abs(matrix), axis=0))


def per_device(view_one, view_two):
    group_count = lax.axis_size("dp")
    batch_rows = view_one.shape[0]
    width = view_one.shape[1]
    total_rows = batch_rows * group_count
    half_width = width // 2
    core_index = lax.axis_index("mp")
    column_start = core_index * half_width
    contract = (((0,), (0,)), ((), ()))
    transposed = (((1,), (1,)), ((), ()))
    column_totals = packed_total(
        (
            jnp.sum(view_one, axis=0, dtype=jnp.float32),
            jnp.sum(view_two, axis=0, dtype=jnp.float32),
        ),
        "dp",
    )
    mean_one = column_totals[0] / total_rows
    mean_two = column_totals[1] / total_rows
    slice_one = lax.dynamic_slice_in_dim(view_one, column_start, half_width, 1)
    slice_two = lax.dynamic_slice_in_dim(view_two, column_start, half_width, 1)
    means_one = lax.dynamic_slice_in_dim(mean_one, column_start, half_width, 0)
    means_two = lax.dynamic_slice_in_dim(mean_two, column_start, half_width, 0)

    def centered(gram, mean_rows, mean_columns):
        return (gram - total_rows * (mean_rows[:, None] * mean_columns[None, :])) / (total_rows - 1)

    gram_one = lax.dot_general(view_one, slice_one, contract, preferred_element_type=jnp.float32)
    gram_two = lax.dot_general(view_two, slice_two, contract, preferred_element_type=jnp.float32)
    gram_cross = lax.dot_general(view_one, slice_two, contract, preferred_element_type=jnp.float32)
    summed = lax.psum((gram_one, gram_two, gram_cross), "dp")
    cov_one = centered(summed[0], mean_one, means_one)
    cov_two = centered(summed[1], mean_two, means_two)
    cov_cross = centered(summed[2], mean_one, means_two)
    bounds = (
        gathered_total(column_peak(cov_one), "mp"),
        gathered_total(column_peak(cov_two), "mp"),
    )
    bound_one = bounds[0] + epsilon
    bound_two = bounds[1] + epsilon
    normed_one = (cov_one / bound_one).astype(jnp.bfloat16)
    normed_two = (cov_two / bound_two).astype(jnp.bfloat16)
    cross_half = cov_cross.astype(jnp.bfloat16)
    cross_full = collect(cross_half, "mp", 1)
    identity_half = (
        jnp.arange(width)[:, None] == (column_start + jnp.arange(half_width))[None, :]
    ).astype(jnp.float32)
    iterate_one = (1.5 * identity_half - 0.5 * normed_one.astype(jnp.float32)).astype(jnp.bfloat16)
    iterate_two = (1.5 * identity_half - 0.5 * normed_two.astype(jnp.float32)).astype(jnp.bfloat16)
    final_one = iterate_one.astype(jnp.float32)
    final_two = iterate_two.astype(jnp.float32)
    for number in range(1, ITERS):
        full_one, full_two = side_by_side((iterate_one, iterate_two), "mp", 1, 0)
        final_one = schulz_step(full_one, normed_one, identity_half)
        final_two = schulz_step(full_two, normed_two, identity_half)
        iterate_one = final_one.astype(jnp.bfloat16)
        iterate_two = final_two.astype(jnp.bfloat16)
    white_half_one = (final_one / jnp.sqrt(bound_one)).astype(jnp.bfloat16)
    white_half_two = (final_two / jnp.sqrt(bound_two)).astype(jnp.bfloat16)
    white_one, white_two = side_by_side((white_half_one, white_half_two), "mp", 1, 0)
    inner_half = jnp.dot(cross_full, white_half_two, preferred_element_type=jnp.float32).astype(
        jnp.bfloat16
    )
    coupling_half = jnp.dot(white_one, inner_half, preferred_element_type=jnp.float32).astype(
        jnp.bfloat16
    )
    coupling = collect(coupling_half, "mp", 1)
    coupling_gram = lax.dot_general(
        coupling, coupling_half, contract, preferred_element_type=jnp.float32
    )
    bound_corr = gathered_total(column_peak(coupling_gram), "mp") + epsilon
    normed_root = (coupling_gram / bound_corr).astype(jnp.bfloat16)
    root_iterate = (1.5 * identity_half - 0.5 * normed_root.astype(jnp.float32)).astype(
        jnp.bfloat16
    )
    final_root = root_iterate.astype(jnp.float32)
    root_full = collect(root_iterate, "mp", 1)
    final_root = schulz_step(root_full, normed_root, identity_half)
    trace_part = jnp.sum(normed_root.astype(jnp.float32) * final_root)
    loss_value = -jnp.sqrt(bound_corr) * over_pieces(trace_part, "mp") / width
    root_half = (final_root / jnp.sqrt(bound_corr)).astype(jnp.bfloat16)
    polar_half = jnp.dot(coupling, root_half, preferred_element_type=jnp.float32).astype(
        jnp.bfloat16
    )
    polar = collect(polar_half, "mp", 1)
    row_share = batch_rows // 2
    row_start = core_index * row_share
    rows_one = lax.dynamic_slice_in_dim(view_one, row_start, row_share, 0)
    rows_two = lax.dynamic_slice_in_dim(view_two, row_start, row_share, 0)
    centered_one = (rows_one.astype(jnp.float32) - mean_one).astype(jnp.bfloat16)
    centered_two = (rows_two.astype(jnp.float32) - mean_two).astype(jnp.bfloat16)
    whitened_one = jnp.dot(centered_one, white_one, preferred_element_type=jnp.float32).astype(
        jnp.bfloat16
    )
    whitened_two = jnp.dot(centered_two, white_two, preferred_element_type=jnp.float32).astype(
        jnp.bfloat16
    )
    aligned_one = jnp.dot(whitened_one, polar, preferred_element_type=jnp.float32)
    aligned_two = lax.dot_general(
        whitened_two, polar, transposed, preferred_element_type=jnp.float32
    )
    difference_one = (
        lax.dot_general(
            aligned_one.astype(jnp.bfloat16),
            coupling,
            transposed,
            preferred_element_type=jnp.float32,
        )
        - aligned_two
    ).astype(jnp.bfloat16)
    difference_two = (
        jnp.dot(aligned_two.astype(jnp.bfloat16), coupling, preferred_element_type=jnp.float32)
        - aligned_one
    ).astype(jnp.bfloat16)
    gradient_one = jnp.dot(difference_one, white_one, preferred_element_type=jnp.float32).astype(
        jnp.bfloat16
    )
    gradient_two = jnp.dot(difference_two, white_two, preferred_element_type=jnp.float32).astype(
        jnp.bfloat16
    )
    return (gradient_one, gradient_two, loss_value)


def solution(mesh):
    in_specs = (P("dp", None), P("dp", None))
    out_specs = (P(("dp", "mp"), None), P(("dp", "mp"), None), P())
    return jax.shard_map(
        per_device, mesh=mesh, in_specs=in_specs, out_specs=out_specs, check_vma=False
    )
```

profile of v0, /device:TPU:1, one launch (start us, length us, event | category | flops | bytes accessed | tf_op | source)
XLA Modules:
  0.0 368.0 jit_solution(17298112653939015617)
XLA Ops:
  7.2 3.6 convolution_bitcast_fusion.1
  10.8 2.1 convolution_bitcast_fusion
  12.9 2.1 convolution_bitcast_fusion.2
  15.5 1.1 broadcast_in_dim.10
  16.5 12.0 %all-to-all-start = ((f32[64,1,2048]{2,1,0:T(1,128)}), f32[64,1,2048]{2,1,0:T(1,128)S(1)}, u32[]{:S(2)}, u32[]{:S(2)}) async-start(f32[64,1,2048]{2,1,0:T(1,128)} %broadcast_in_dim.10), calls=%async_computation | async-start | bytes 1048576 | tf_op jit(solution)/shard_map/all_to_all | solution.py:14
  28.6 0.6 dynamic-slice
  29.2 16.9 %all-to-all-done = f32[64,1,2048]{2,1,0:T(1,128)S(1)} async-done(((f32[64,1,2048]{2,1,0:T(1,128)}), f32[64,1,2048]{2,1,0:T(1,128)S(1)}, u32[]{:S(2)}, u32[]{:S(2)}) %all-to-all-start) | async-done | bytes 524320 | tf_op jit(solution)/shard_map/all_to_all | solution.py:14
  46.1 0.3 reduce_sum.74
  46.5 124.9 %all-reduce.8.cloned.1.call-done = (f32[1024,512]{0,1:T(8,128)}, f32[1024,512]{0,1:T(8,128)}, f32[1024,512]{0,1:T(8,128)}) async-done(((f32[1024,512]{0,1:T(8,128)}, f32[1024,512]{0,1:T(8,128)}, f32[1024,512]{0,1:T(8,128)}), (f32[1024,512]{0,1:T(8,128)}, f32[1024,512]{0,1:T(8,128)}, f32[1024,512]{0,1:T(8,128)})) %all-reduce.8.cloned.1.call-update) | async-done | bytes 6291472 | tf_op jit(solution)/shard_map/psum | solution.py:100
  171.5 3.4 abs_reduce_fusion.1
  174.8 0.6 reduce_max.54
  175.4 0.6 reduce_max.56
  176.0 1.4 dynamic-update-slice
  177.4 1.4 dynamic-update-slice.1
  178.8 3.6 all-reduce.5
  182.4 0.6 reduce_max.55
  183.0 0.6 reduce_max.57
  184.9 4.3 %fusion.1 = (bf16[1024,512]{0,1:T(8,128)(2,1)S(1)}, bf16[1024,512]{0,1:T(8,128)(2,1)}, bf16[1024,512]{0,1:T(8,128)(2,1)}, bf16[1024,512]{0,1:T(8,128)(2,1)S(1)}, bf16[1024,512]{0,1:T(8,128)(2,1)}) fusion(s32[512]{0:T(512)S(1)} %iota_add_fusion, f32[]{:T(128)S(6)} %add.39, f32[1024,512]{0,1:T(8,128)} %get-tuple-element.4, f32[512]{0:T(512)S(1)} %dynamic_slice.20, ...), kind=kLoop, calls=%fused_computation.11 | loop fusion | flops 14155776 | bytes 11548680 | tf_op jit(solution)/shard_map/convert_element_type | solution.py:117
  189.3 1.5 pad_maximum_fusion
  191.0 15.9 %all-gather.4.cloned.1.call-done = bf16[2048,1024]{0,1:T(8,128)(2,1)} async-done(((bf16[2048,512]{0,1:T(8,128)(2,1)}), bf16[2048,1024]{0,1:T(8,128)(2,1)}) %all-gather.4.cloned.1.call-update) | async-done | bytes 4194320 | tf_op jit(solution)/shard_map/all_gather | solution.py:50
  206.9 3.9 %fusion.39 = bf16[1024,512]{1,0:T(8,128)(2,1)} fusion(bf16[1024,512]{0,1:T(8,128)(2,1)S(1)} %copy-done.14, bf16[2048,1024]{0,1:T(8,128)(2,1)} %all-gather.4.cloned.1.call-done), kind=kOutput, calls=%fused_computation.70 | convolution fusion | flops 1074266112 | bytes 4194304 | tf_op jit(solution)/shard_map/dot_general | solution.py:59
  210.8 5.0 %fusion.42 = bf16[1024,512]{1,0:T(8,128)(2,1)S(1)} fusion(bf16[2048,1024]{0,1:T(8,128)(2,1)} %all-gather.4.cloned.1.call-done, bf16[1024,512]{1,0:T(8,128)(2,1)} %fusion.39, s32[512]{0:T(512)S(1)} %iota_add_fusion), kind=kOutput, calls=%fused_computation.71 | convolution fusion | flops 2150629376 | bytes 6293504 | tf_op jit(solution)/shard_map/dot_general | solution.py:63
  215.8 3.9 %fusion.45 = bf16[1024,512]{1,0:T(8,128)(2,1)} fusion(bf16[1024,512]{0,1:T(8,128)(2,1)S(1)} %copy-done.12, bf16[2048,1024]{0,1:T(8,128)(2,1)} %all-gather.4.cloned.1.call-done), kind=kOutput, calls=%fused_computation.72 | convolution fusion | flops 1074266112 | bytes 4194304 | tf_op jit(solution)/shard_map/dot_general | solution.py:59
  219.7 4.9 %fusion.48 = bf16[1024,512]{1,0:T(8,128)(2,1)S(1)} fusion(bf16[2048,1024]{0,1:T(8,128)(2,1)} %all-gather.4.cloned.1.call-done, bf16[1024,512]{1,0:T(8,128)(2,1)} %fusion.45, s32[512]{0:T(512)S(1)} %iota_add_fusion), kind=kOutput, calls=%fused_computation.73 | convolution fusion | flops 2150629376 | bytes 6293504 | tf_op jit(solution)/shard_map/dot_general | solution.py:63
  224.6 1.5 pad_maximum_fusion.1
  226.5 17.5 %all-gather.6.cloned.1.call-done = bf16[2048,1024]{1,0:T(8,128)(2,1)} async-done(((bf16[2048,512]{1,0:T(8,128)(2,1)}), bf16[2048,1024]{1,0:T(8,128)(2,1)}) %all-gather.6.cloned.1.call-update) | async-done | bytes 4194320 | tf_op jit(solution)/shard_map/all_gather | solution.py:50
  244.0 4.0 %fusion.51 = bf16[1024,512]{1,0:T(8,128)(2,1)} fusion(bf16[1024,512]{0,1:T(8,128)(2,1)S(1)} %copy-done.15, bf16[2048,1024]{1,0:T(8,128)(2,1)} %all-gather.6.cloned.1.call-done), kind=kOutput, calls=%fused_computation.74 | convolution fusion | flops 1074266112 | bytes 4194304 | tf_op jit(solution)/shard_map/dot_general | solution.py:59
  248.0 2.3 fusion.54
  250.3 4.9 %divide_convert_fusion.3 = bf16[1024,512]{1,0:T(8,128)(2,1)S(1)} fusion(f32[]{:T(128)S(6)} %sqrt.10, bf16[2048,1024]{1,0:T(8,128)(2,1)} %all-gather.6.cloned.1.call-done, bf16[1024,512]{1,0:T(8,128)(2,1)} %fusion.51, s32[512]{0:T(512)S(1)} %iota_add_fusion), kind=kOutput, calls=%fused_computation.27 | convolution fusion | flops 2151153664 | bytes 6293508 | tf_op jit(solution)/shard_map/dot_general | solution.py:63
  255.2 4.9 %divide_convert_fusion.2 = bf16[1024,512]{1,0:T(8,128)(2,1)S(1)} fusion(f32[]{:T(128)S(6)} %sqrt.11, bf16[2048,1024]{1,0:T(8,128)(2,1)} %all-gather.6.cloned.1.call-done, bf16[1024,512]{1,0:T(8,128)(2,1)} %fusion.54, s32[512]{0:T(512)S(1)} %iota_add_fusion), kind=kOutput, calls=%fused_computation.26 | convolution fusion | flops 2151153664 | bytes 6293508 | tf_op jit(solution)/shard_map/dot_general | solution.py:63
  260.1 1.0 copy-done.11
  261.1 1.5 pad_maximum_fusion.2
  262.6 1.2 copy-done.3
  264.1 5.3 %all_to_all.26 = bf16[2,1024,512]{1,2,0:T(8,128)(2,1)S(1)} all-to-all(bf16[2,1024,512]{1,2,0:T(8,128)(2,1)S(1)} %broadcast_in_dim.11), channel_id=1, replica_groups=mesh['dp'=64,'mp'=2] {'mp'}, dimensions={0} | all-to-all | bytes 4194304 | tf_op jit(solution)/shard_map/all_to_all | solution.py:14
  269.3 11.1 %all-gather.8.cloned.1.call-done = bf16[2048,1024]{1,0:T(8,128)(2,1)} async-done(((bf16[2048,512]{1,0:T(8,128)(2,1)}), bf16[2048,1024]{1,0:T(8,128)(2,1)}) %all-gather.8.cloned.1.call-update) | async-done | bytes 4194320 | tf_op jit(solution)/shard_map/all_gather | solution.py:50
  280.5 5.2 %fusion.57 = bf16[1024,512]{1,0:T(8,128)(2,1)} fusion(bf16[2048,1024]{1,0:T(8,128)(2,1)} %all-gather.8.cloned.1.call-done, bf16[1024,1024]{0,1:T(8,128)(2,1)S(1)} %bitcast.54, bf16[1024,512]{1,0:T(8,128)(2,1)} %copy-done.11), kind=kOutput, calls=%fused_computation.76 | convolution fusion | flops 2148532224 | bytes 6291456 | tf_op jit(solution)/shard_map/dot_general | solution.py:133
  285.7 1.5 copy.27
  287.5 5.4 %all_to_all.27 = bf16[2,1024,512]{1,2,0:T(8,128)(2,1)S(1)} all-to-all(bf16[2,1024,512]{1,2,0:T(8,128)(2,1)S(1)} %broadcast_in_dim.12), channel_id=1, replica_groups=mesh['dp'=64,'mp'=2] {'mp'}, dimensions={0} | all-to-all | bytes 4194304 | tf_op jit(solution)/shard_map/all_to_all | solution.py:14
  292.9 2.6 abs_reduce_fusion
  295.4 0.6 reduce_max.58
  296.0 1.4 dynamic-update-slice.2
  297.4 1.9 copy.28
  299.4 2.5 all-reduce.2
  301.9 0.6 reduce_max.59
  303.2 1.5 fusion.7
  304.7 0.3 broadcast_in_dim.13
  305.0 6.7 %all_to_all.28 = bf16[2,1024,512]{1,2,0:T(8,128)(2,1)} all-to-all(bf16[2,1024,512]{1,2,0:T(8,128)(2,1)S(1)} %broadcast_in_dim.13), channel_id=1, replica_groups=mesh['dp'=64,'mp'=2] {'mp'}, dimensions={0} | all-to-all | bytes 4194304 | tf_op jit(solution)/shard_map/all_to_all | solution.py:14
  311.7 4.7 %fusion.8 = bf16[1024,512]{0,1:T(8,128)(2,1)S(1)} fusion(bf16[1024,1024]{0,1:T(8,128)(2,1)} %bitcast.55, s32[512]{0:T(512)S(1)} %iota_add_fusion, bf16[1024,512]{0,1:T(8,128)(2,1)S(1)} %copy-done.2), kind=kOutput, calls=%fused_computation.18 | convolution fusion | flops 2150629376 | bytes 4196352 | tf_op jit(solution)/shard_map/dot_general | solution.py:61
  316.4 4.2 %fusion.127 = f32[1024,512]{1,0:T(8,128)} fusion(bf16[1024,1024]{0,1:T(8,128)(2,1)} %bitcast.56, bf16[1024,512]{0,1:T(8,128)(2,1)S(1)} %fusion.8), kind=kOutput, calls=%fused_computation.123 | convolution fusion | flops 1073741824 | bytes 5242880 | tf_op jit(solution)/shard_map/dot_general | solution.py:63
  320.7 1.9 copy.31
  322.6 2.5 fusion
  325.1 2.9 convolution_convert_fusion
  328.0 1.4 dynamic-update-slice.3
  329.4 2.5 all-reduce.3
  331.9 0.5 copy.30
  332.5 1.6 broadcast_in_dim.14
  334.1 4.1 %all-to-all-start.4 = ((bf16[2,1024,512]{1,2,0:T(8,128)(2,1)}), bf16[2,1024,512]{1,2,0:T(8,128)(2,1)S(1)}, u32[]{:S(2)}, u32[]{:S(2)}) async-start(bf16[2,1024,512]{1,2,0:T(8,128)(2,1)} %broadcast_in_dim.14), calls=%async_computation.4 | async-start | bytes 4194304 | tf_op jit(solution)/shard_map/all_to_all | solution.py:14
  338.2 0.6 reduce_sum.79
  339.4 1.2 all-to-all-done.4
  340.7 1.3 copy-done.9
  342.0 4.5 %fusion.78 = f32[256,1024]{1,0:T(8,128)} fusion(bf16[1024,1024]{0,1:T(8,128)(2,1)} %bitcast.52, bf16[2048,1024]{1,0:T(8,128)(2,1)} %all-gather.8.cloned.1.call-done, f32[1024]{0:T(1024)S(1)} %get-tuple-element.14, bf16[512,1024]{1,0:T(8,128)(2,1)S(1)} %copy-done.1, s32[]{:T(128)S(6)} %select_n.4), kind=kOutput, calls=%fused_computation.89 | convolution fusion | flops 1074790400 | bytes 5771268 | tf_op jit(solution)/shard_map/dot_general | solution.py:167
  346.5 4.6 %fusion.75 = f32[256,1024]{1,0:T(8,128)} fusion(bf16[1024,1024]{0,1:T(8,128)(2,1)} %bitcast.53, bf16[2048,1024]{1,0:T(8,128)(2,1)} %all-gather.8.cloned.1.call-done, f32[1024]{0:T(1024)S(1)} %get-tuple-element.15, bf16[512,1024]{1,0:T(8,128)(2,1)S(1)} %copy-done.5, s32[]{:T(128)S(6)} %select_n.4), kind=kOutput, calls=%fused_computation.88 | convolution fusion | flops 1074790400 | bytes 5771268 | tf_op jit(solution)/shard_map/dot_general | solution.py:168
  351.2 4.8 %fusion.69 = bf16[256,1024]{1,0:T(8,128)(2,1)} fusion(bf16[2048,1024]{1,0:T(8,128)(2,1)} %all-gather.8.cloned.1.call-done, f32[256,1024]{1,0:T(8,128)S(1)} %copy-done.18, bf16[1024,1024]{0,1:T(8,128)(2,1)} %bitcast.49, f32[256,1024]{1,0:T(8,128)} %fusion.75), kind=kOutput, calls=%fused_computation.85 | convolution fusion | flops 1074790400 | bytes 6815744 | tf_op jit(solution)/shard_map/dot_general | solution.py:187
  356.0 4.0 %fusion.63 = bf16[256,1024]{1,0:T(8,128)(2,1)} fusion(bf16[2048,1024]{1,0:T(8,128)(2,1)} %all-gather.8.cloned.1.call-done, f32[256,1024]{1,0:T(8,128)} %fusion.75, bf16[1024,1024]{0,1:T(8,128)(2,1)S(1)} %bitcast.51, f32[256,1024]{1,0:T(8,128)S(1)} %copy-done.18), kind=kOutput, calls=%fused_computation.83 | convolution fusion | flops 1074790400 | bytes 6815744 | tf_op jit(solution)/shard_map/dot_general | solution.py:184
  (56 shorter events, 1.7 us)
Async XLA Ops:
  7.2 164.3 %all-reduce.8.cloned.1.call-start = ((), (), s32[]{:S(2)}) async-start(), calls=%async_computation.8 | async-start | bytes 12582912 | tf_op jit(solution)/shard_map/psum | solution.py:100
  7.2 3.6 copy-start.1
  7.2 3.6 copy-start.4
  15.1 13.5 %copy-start.17 = (u32[128]{0:T(128)S(1)}, u32[128]{0:T(128)}, u32[]{:S(2)}) copy-start(u32[128]{0:T(128)} %constant.39) | copy-start | bytes 1540
  16.5 29.5 %all-to-all-start = ((f32[64,1,2048]{2,1,0:T(1,128)}), f32[64,1,2048]{2,1,0:T(1,128)S(1)}, u32[]{:S(2)}, u32[]{:S(2)}) async-start(f32[64,1,2048]{2,1,0:T(1,128)} %broadcast_in_dim.10), calls=%async_computation | async-start | bytes 1048576 | tf_op jit(solution)/shard_map/all_to_all | solution.py:14
  28.5 178.4 %all-gather.4.cloned.1.call-start = ((), (), s32[]{:S(2)}) async-start(), calls=%async_computation.5 | async-start | bytes 6291456 | tf_op jit(solution)/shard_map/all_gather | solution.py:50
  171.4 13.4 %copy-start = (f32[1024,512]{0,1:T(8,128)S(1)}, f32[1024,512]{0,1:T(8,128)}, u32[]{:S(2)}) copy-start(f32[1024,512]{0,1:T(8,128)} %get-tuple-element.3) | copy-start | bytes 6291460
  190.8 16.2 %copy-start.14 = (bf16[1024,512]{0,1:T(8,128)(2,1)S(1)}, bf16[1024,512]{0,1:T(8,128)(2,1)}, u32[]{:S(2)}) copy-start(bf16[1024,512]{0,1:T(8,128)(2,1)} %get-tuple-element.11) | copy-start | bytes 3145732
  190.8 53.2 %all-gather.6.cloned.1.call-start = ((), (), s32[]{:S(2)}) async-start(), calls=%async_computation.6 | async-start | bytes 6291456 | tf_op jit(solution)/shard_map/all_gather | solution.py:50
  210.8 5.0 %copy-start.12 = (bf16[1024,512]{0,1:T(8,128)(2,1)S(1)}, bf16[1024,512]{0,1:T(8,128)(2,1)}, u32[]{:S(2)}) copy-start(bf16[1024,512]{0,1:T(8,128)(2,1)} %get-tuple-element.18) | copy-start | bytes 3145732
  226.1 17.9 %copy-start.15 = (bf16[1024,512]{0,1:T(8,128)(2,1)S(1)}, bf16[1024,512]{0,1:T(8,128)(2,1)}, u32[]{:S(2)}) copy-start(bf16[1024,512]{0,1:T(8,128)(2,1)} %get-tuple-element.11) | copy-start | bytes 3145732
  226.1 54.3 %all-gather.8.cloned.1.call-start = ((), (), s32[]{:S(2)}) async-start(), calls=%async_computation.7 | async-start | bytes 6291456 | tf_op jit(solution)/shard_map/all_gather | solution.py:50
  226.5 21.6 %copy-start.13 = (bf16[1024,512]{0,1:T(8,128)(2,1)S(1)}, bf16[1024,512]{0,1:T(8,128)(2,1)}, u32[]{:S(2)}) copy-start(bf16[1024,512]{0,1:T(8,128)(2,1)} %get-tuple-element.18) | copy-start | bytes 3145732
  244.0 4.0 %copy-start.16 = (bf16[2048,1024]{1,0:T(8,128)(2,1)S(1)}, bf16[2048,1024]{1,0:T(8,128)(2,1)}, u32[]{:S(2)}) copy-start(bf16[2048,1024]{1,0:T(8,128)(2,1)} %all-gather.6.cloned.1.call-done) | copy-start | bytes 12582916
  260.1 1.0 copy-start.11
  262.6 1.2 copy-start.3
  287.4 5.4 %copy-start.10 = (bf16[1024,512]{1,0:T(8,128)(2,1)S(1)}, bf16[1024,512]{1,0:T(8,128)(2,1)}, u32[]{:S(2)}) copy-start(bf16[1024,512]{1,0:T(8,128)(2,1)} %fusion.57) | copy-start | bytes 3145732
  292.8 2.6 copy-start.6
  305.0 6.7 %copy-start.2 = (bf16[1024,512]{0,1:T(8,128)(2,1)S(1)}, bf16[1024,512]{0,1:T(8,128)(2,1)}, u32[]{:S(2)}) copy-start(bf16[1024,512]{0,1:T(8,128)(2,1)} %get-tuple-element.9) | copy-start | bytes 3145732
  322.6 2.5 copy-start.7
  334.1 6.6 %all-to-all-start.4 = ((bf16[2,1024,512]{1,2,0:T(8,128)(2,1)}), bf16[2,1024,512]{1,2,0:T(8,128)(2,1)S(1)}, u32[]{:S(2)}, u32[]{:S(2)}) async-start(bf16[2,1024,512]{1,2,0:T(8,128)(2,1)} %broadcast_in_dim.14), calls=%async_computation.4 | async-start | bytes 4194304 | tf_op jit(solution)/shard_map/all_to_all | solution.py:14
  340.7 1.3 copy-start.9
  342.0 4.5 %copy-start.5 = (bf16[512,1024]{1,0:T(8,128)(2,1)S(1)}, bf16[512,1024]{1,0:T(8,128)(2,1)}, u32[]{:S(2)}) copy-start(bf16[512,1024]{1,0:T(8,128)(2,1)} %param.3) | copy-start | bytes 3145732
  346.5 4.6 %copy-start.18 = (f32[256,1024]{1,0:T(8,128)S(1)}, f32[256,1024]{1,0:T(8,128)}, u32[]{:S(2)}) copy-start(f32[256,1024]{1,0:T(8,128)} %fusion.78) | copy-start | bytes 3145732
  351.2 4.8 %copy-start.8 = (bf16[2,1024,512]{1,2,0:T(8,128)(2,1)S(1)}, bf16[2,1024,512]{1,2,0:T(8,128)(2,1)}, u32[]{:S(2)}) copy-start(bf16[2,1024,512]{1,2,0:T(8,128)(2,1)} %copy-done.6) | copy-start | bytes 6291460
Sparse Core Ops, SparseCore 0:
  15.2 156.2 all-reduce.7
  190.9 15.9 all-gather.3
  226.2 17.6 all-gather.5
  262.7 17.6 all-gather.7
where the time goes:
time: 374 us; the launch traced here: 368 us
  waiting for transfers between devices  188 us (50%)
  matrix products  79.2 us (21%)
  blocking collectives  25.9 us (7%)
  other arithmetic  21.1 us (6%)
  local copies, waits for them, and re-layouts  19.2 us (5%)
  between operations  18.3 us (5%)
  starting transfers between devices  16.6 us (4%)
    psum x1, waiting for transfers between devices, per_device(): summed = lax.psum((gram_one, gram_two, gram_cross), 'dp')  125 us
    all_gather x3, waiting for transfers between devices, side_by_side(): lax.all_gather(both, axis, axis=dim, tiled=True)  44.6 us
    dot_general x5, matrix products, schulz_step(): return jnp.dot(full, target, preferred_element_type=jnp.float32)  24 us
    all_to_all x2, waiting for transfers between devices, copy_for_each(): lax.all_to_all(jnp.broadcast_to(x[None], (length, *x.shape)), axis, 0, 0,...  18.2 us
    all_to_all x3, blocking collectives, copy_for_each(): lax.all_to_all(jnp.broadcast_to(x[None], (length, *x.shape)), axis, 0, 0,...  17.4 us
    all_to_all x2, starting transfers between devices, copy_for_each(): lax.all_to_all(jnp.broadcast_to(x[None], (length, *x.shape)), axis, 0, 0,...  16.1 us
    dot_general x4, matrix products, schulz_step(): jnp.dot(full, normed_half, preferred_element_type=jnp.float32)  14 us
    unnamed x47, local copies, waits for them, and re-layouts  9.77 us
  transfers between devices with their start and end apart: 6, of which 6 were waited for; matrix products, arithmetic and copies ran while one was open for 1% of the time, Pallas kernels for 0%

commit v1 on v0

v1 whole, which is shorter than its diff:
```python
import jax
import jax.numpy as jnp
from jax import lax
from jax.experimental import pallas as pl
from jax.experimental.pallas import tpu as pltpu
from jax.sharding import PartitionSpec as P

MESH = pl.DeviceIdType.MESH
F32, BF16 = jnp.float32, jnp.bfloat16
EPS = 1e-6
RING = 4
WIDTH = 1024
BLK = 256
NBLK = WIDTH // BLK
COLS = (((0,), (0,)), ((), ()))
ROWS = (((1,), (1,)), ((), ()))
JOBS = ((0, 2, 0), (128, 2, 1), (256, 1, 2), (320, 1, 0), (384, 1, 1), (448, 2, 2))
GRAM, CROSS = (0, 1, 2), (3, 4, 5)
AXES = ((0, 1, 2), (1, 2, 0), (2, 0, 1))
OFFSETS = (0, 32, 64, 80, 96, 112)


def dot(a, b):
    return jnp.dot(a, b, preferred_element_type=F32)


def kernel(
    total_rows, one_hbm, two_hbm, grad_one, grad_two, loss_ref,
    vs, pb, r1, r2, r3, sb, sr, mb, cb, xo, an, z, zn, w, xm, cm, ct, cg, pol, p_s, t_s,
    local_sem, send_sem, recv_sem, sum_send, sum_recv, w_send, w_recv, x_send, x_recv,
):
    dp, core = lax.axis_index("dp"), lax.axis_index("mp")
    at = (dp // 16, (dp // 4) % 4, dp % 4)
    rows = vs.shape[1]

    def peer(axis, k):
        place = list(at)
        place[axis] = (place[axis] + k) % RING
        return (place[0] * 16 + place[1] * 4 + place[2], core)

    partner = (dp, 1 - core)
    loads = [
        pltpu.make_async_copy(src, vs.at[i], local_sem.at[i])
        for i, src in enumerate((one_hbm, two_hbm))
    ]
    for load in loads:
        load.start()
    barrier = pltpu.get_barrier_semaphore()
    for axis in range(3):
        for k in range(1, RING):
            pl.semaphore_signal(barrier, inc=1, device_id=peer(axis, k), device_id_type=MESH)
    pl.semaphore_signal(barrier, inc=1, device_id=partner, device_id_type=MESH)
    for load in loads:
        load.wait()

    ones = jnp.ones((8, rows), BF16)
    for v in range(2):
        s = dot(ones, vs[v])
        for k in range(8):
            sb[0, v * 8 + k : v * 8 + k + 1, :] = s[0:1, 128 * k : 128 * k + 128]
    tile = 0
    for bi in range(NBLK):
        g = lax.dot_general(
            vs[core, :, BLK * bi : BLK * bi + BLK], vs[core, :, BLK * bi :], COLS,
            preferred_element_type=F32,
        )
        for h in range(g.shape[1] // 128):
            pb[tile : tile + 16] = g[:, 128 * h : 128 * h + 128].reshape(16, 16, 128)
            tile += 16
    for r in range(2):
        start = pl.multiple_of(core * 512 + r * BLK, BLK)
        g = lax.dot_general(
            vs[0, :, pl.ds(start, BLK)], vs[1], COLS, preferred_element_type=F32
        )
        for h in range(8):
            pb[tile : tile + 16] = g[:, 128 * h : 128 * h + 128].reshape(16, 16, 128)
            tile += 16

    pl.semaphore_wait(barrier, 10)
    sends = []

    bases = []
    for base, t, order in JOBS:
        b = [jnp.int32(base)]
        for p in range(3):
            b.append(b[-1] + at[AXES[order][p]] * (t * 4 ** (2 - p)))
        bases.append(b)
    slots = (r1, r2, r3)

    for p in range(3):
        started = []
        copies = []
        for k in (2, 1, 3):
            copy = pltpu.make_async_remote_copy(
                src_ref=sb.at[p], dst_ref=sr.at[p, k - 1],
                send_sem=sum_send.at[p, k - 1], recv_sem=sum_recv.at[p, k - 1],
                device_id=peer(p, k), device_id_type=MESH,
            )
            copy.start()
            copies.append(copy)
        for k in (2, 1, 3):
            for j, (base, t, order) in enumerate(JOBS):
                n = t * 4 ** (2 - p)
                axis = AXES[order][p]
                to = (at[axis] + k) % RING
                copy = pltpu.make_async_remote_copy(
                    src_ref=pb.at[pl.ds(bases[j][p] + to * n, n)],
                    dst_ref=slots[p].at[k - 1, pl.ds(OFFSETS[j] // 4**p, n)],
                    send_sem=send_sem.at[p, j, k - 1], recv_sem=recv_sem.at[p, j, k - 1],
                    device_id=peer(axis, k), device_id_type=MESH,
                )
                copy.start()
                started.append((j, copy))
        for copy in copies:
            copy.wait_recv()
        sb[p + 1] = sb[p] + sr[p, 0] + sr[p, 1] + sr[p, 2]
        for j, (base, t, order) in enumerate(JOBS):
            for i, copy in started:
                if i == j:
                    copy.wait_recv()
            n = t * 4 ** (2 - p)
            mine = pl.ds(bases[j][p + 1], n)
            got = slice(OFFSETS[j] // 4**p, OFFSETS[j] // 4**p + n)
            pb[mine] = pb[mine] + slots[p][0, got] + slots[p][1, got] + slots[p][2, got]
        sends += copies + [copy for _, copy in started]

    for i in range(16):
        mb[i] = jnp.broadcast_to(sb[3, i : i + 1, :] / total_rows, (8, 128))
    lane = lax.broadcasted_iota(jnp.int32, (8, 128), 1)
    sub = lax.broadcasted_iota(jnp.int32, (8, 128), 0)

    def center(j):
        base, t, order = JOBS[j]
        for q in range(t):
            tile = bases[j][3] + q
            if j in GRAM:
                hb = tile // 16
                blk = hb // 2
                ge4 = jnp.where(blk >= 4, 1, 0)
                ge7 = jnp.where(blk >= 7, 1, 0)
                ge9 = jnp.where(blk >= 9, 1, 0)
                bi = ge4 + ge7 + ge9
                bj = blk - 4 * ge4 - 3 * ge7 - 2 * ge9 + bi
                row = bi * BLK + (tile % 16) * 16
                column = bj * 2 + hb % 2
                row_view, column_view = core, core
            else:
                hb = (tile - 320) // 16
                row = core * 512 + (hb // 8) * BLK + (tile % 16) * 16
                column = hb % 8
                row_view, column_view = 0, 1
            across = mb[column_view * 8 + column]
            down = mb[row_view * 8 + row // 128]
            halves = []
            for h in range(2):
                at_row = lane == (row % 128) + h * 8 + sub
                col = jnp.sum(jnp.where(at_row, down, 0.0), axis=1, keepdims=True)
                raw = pb[tile, h * 8 : h * 8 + 8, :]
                halves.append((raw - total_rows * (col * across)) * (1.0 / (total_rows - 1)))
            cb[tile] = jnp.concatenate(halves, axis=0).astype(BF16)

    def gather_start(p, group):
        out = []
        for k in (2, 1, 3):
            for j in group:
                base, t, order = JOBS[j]
                part = cb.at[pl.ds(bases[j][p + 1], t * 4 ** (2 - p))]
                copy = pltpu.make_async_remote_copy(
                    src_ref=part, dst_ref=part,
                    send_sem=send_sem.at[3 + p, j, k - 1], recv_sem=recv_sem.at[3 + p, j, k - 1],
                    device_id=peer(AXES[order][p], k), device_id_type=MESH,
                )
                copy.start()
                out.append(copy)
        return out

    def gather_wait(copies):
        for copy in copies:
            copy.wait_recv()
        sends.extend(copies)

    for j in range(6):
        center(j)
    for p in (2, 1, 0):
        flight = gather_start(p, GRAM)
        if p == 0:
            cross_flight = gather_start(2, CROSS)
        gather_wait(flight)

    tile = 0
    for bi in range(NBLK):
        for bj in range(bi, NBLK):
            for h in range(2):
                part = cb[tile : tile + 16].reshape(BLK, 128)
                left = BLK * bj + 128 * h
                an[BLK * bi : BLK * bi + BLK, left : left + 128] = part
                if bi != bj:
                    an[left : left + 128, BLK * bi : BLK * bi + BLK] = part.T
                tile += 16

    def columns(j):
        return pl.ds(pl.multiple_of(j * BLK, BLK), BLK)

    def identity(j):
        r = lax.broadcasted_iota(jnp.int32, (WIDTH, BLK), 0)
        c = lax.broadcasted_iota(jnp.int32, (WIDTH, BLK), 1)
        return jnp.where(r == c + j * BLK, 1.5, 0.0)

    def peak(j, top):
        return jnp.maximum(top, jnp.max(jnp.sum(jnp.abs(an[:, columns(j)].astype(F32)), axis=0)))

    bound = lax.fori_loop(0, NBLK, peak, jnp.float32(0.0)) + EPS
    scale = 1.0 / bound
    white_scale = lax.rsqrt(bound)

    def norm(j, _):
        a = (an[:, columns(j)].astype(F32) * scale).astype(BF16)
        an[:, columns(j)] = a
        z[:, columns(j)] = (identity(j) - 0.5 * a.astype(F32)).astype(BF16)
        return 0

    lax.fori_loop(0, NBLK, norm, 0)
    gather_wait(cross_flight)
    cross_flight = gather_start(1, CROSS)

    def step(it, j):
        p_s[...] = dot(it[...], an[:, columns(j)]).astype(BF16)
        t_s[...] = (identity(j) - 0.5 * dot(it[...], p_s[...])).astype(BF16)
        return dot(it[...], t_s[...])

    def first(j, _):
        zn[:, columns(j)] = step(z, j).astype(BF16)
        return 0

    lax.fori_loop(0, NBLK, first, 0)
    gather_wait(cross_flight)
    cross_flight = gather_start(0, CROSS)

    def white_copy(j):
        part = w.at[core, :, columns(j)]
        return pltpu.make_async_remote_copy(
            src_ref=part, dst_ref=part, send_sem=w_send.at[j], recv_sem=w_recv.at[j],
            device_id=partner, device_id_type=MESH,
        )

    def second(j, _):
        w[core, :, columns(j)] = (step(zn, j) * white_scale).astype(BF16)
        white_copy(j).start()
        return 0

    lax.fori_loop(0, NBLK, second, 0)
    gather_wait(cross_flight)
    cross_copy = pltpu.make_async_remote_copy(
        src_ref=cb.at[pl.ds(320, 256)], dst_ref=xo, send_sem=x_send, recv_sem=x_recv,
        device_id=partner, device_id_type=MESH,
    )
    cross_copy.start()

    def place(src, first_tile, half):
        for r in range(2):
            for q in range(8):
                t0 = first_tile + (r * 8 + q) * 16
                xm[pl.ds(pl.multiple_of(half * 512 + r * BLK, BLK), BLK), 128 * q : 128 * q + 128] = (
                    src[t0 : t0 + 16].reshape(BLK, 128)
                )

    place(cb, 320, core)
    share = rows // 2
    mine = pl.ds(pl.multiple_of(core * share, share), share)
    centered = []
    for v in range(2):
        mean = jnp.concatenate([mb[v * 8 + k][0:1, :] for k in range(8)], axis=1)
        centered.append((vs[v, mine, :].astype(F32) - mean).astype(BF16))
    for j in range(NBLK):
        copy = white_copy(j)
        copy.wait_recv()
        sends.append(copy)
    whitened = [dot(centered[v], w[v]).astype(BF16) for v in range(2)]
    cross_copy.wait_recv()
    sends.append(cross_copy)
    place(xo, 0, 1 - core)

    def couple(j, _):
        p_s[...] = dot(xm[...], w[1, :, columns(j)]).astype(BF16)
        c = dot(w[0], p_s[...]).astype(BF16)
        cm[:, columns(j)] = c
        ct[columns(j), :] = c.T
        return 0

    lax.fori_loop(0, NBLK, couple, 0)

    def root_gram(j, top):
        g = dot(ct[...], cm[:, columns(j)])
        cg[:, columns(j)] = g
        return jnp.maximum(top, jnp.max(jnp.sum(jnp.abs(g), axis=0)))

    bound_root = lax.fori_loop(0, NBLK, root_gram, jnp.float32(0.0)) + EPS
    root_scale = 1.0 / bound_root
    inverse_scale = lax.rsqrt(bound_root)

    def root_norm(j, _):
        a = (cg[:, columns(j)] * root_scale).astype(BF16)
        an[:, columns(j)] = a
        z[:, columns(j)] = (identity(j) - 0.5 * a.astype(F32)).astype(BF16)
        return 0

    lax.fori_loop(0, NBLK, root_norm, 0)

    def root(j, trace):
        f = step(z, j)
        p_s[...] = (f * inverse_scale).astype(BF16)
        trace = trace + jnp.sum(an[:, columns(j)].astype(F32) * f)
        pol[:, columns(j)] = dot(cm[...], p_s[...]).astype(BF16)
        return trace

    trace = lax.fori_loop(0, NBLK, root, jnp.float32(0.0))
    loss_ref[...] = jnp.full(loss_ref.shape, -(bound_root * inverse_scale) * trace / WIDTH, F32)

    aligned_one = dot(whitened[0], pol[...])
    aligned_two = lax.dot_general(whitened[1], pol[...], ROWS, preferred_element_type=F32)
    difference_one = (dot(aligned_one.astype(BF16), ct[...]) - aligned_two).astype(BF16)
    difference_two = (dot(aligned_two.astype(BF16), cm[...]) - aligned_one).astype(BF16)
    grad_one[...] = dot(difference_one, w[0]).astype(BF16)
    grad_two[...] = dot(difference_two, w[1]).astype(BF16)
    for copy in sends:
        copy.wait_send()


def per_device(view_one, view_two):
    rows, width = view_one.shape
    total_rows = rows * lax.axis_size("dp")

    def body(*refs):
        kernel(total_rows, *refs)

    square = pltpu.VMEM((width, width), BF16)
    tall = pltpu.VMEM((width, BLK), BF16)
    dma = pltpu.SemaphoreType.DMA
    grad_one, grad_two, loss = pl.pallas_call(
        body,
        name="cca",
        out_shape=(
            jax.ShapeDtypeStruct((rows // 2, width), BF16),
            jax.ShapeDtypeStruct((rows // 2, width), BF16),
            jax.ShapeDtypeStruct((8, 128), F32),
        ),
        in_specs=[pl.BlockSpec(memory_space=pl.ANY)] * 2,
        out_specs=[pl.BlockSpec(memory_space=pltpu.VMEM)] * 3,
        scratch_shapes=[
            pltpu.VMEM((2, rows, width), BF16),
            pltpu.VMEM((576, 16, 128), F32),
            pltpu.VMEM((3, 144, 16, 128), F32),
            pltpu.VMEM((3, 36, 16, 128), F32),
            pltpu.VMEM((3, 9, 16, 128), F32),
            pltpu.VMEM((4, 16, 128), F32),
            pltpu.VMEM((3, 3, 16, 128), F32),
            pltpu.VMEM((16, 8, 128), F32),
            pltpu.VMEM((576, 16, 128), BF16),
            pltpu.VMEM((256, 16, 128), BF16),
            square, square, square,
            pltpu.VMEM((2, width, width), BF16),
            square, square, square,
            pltpu.VMEM((width, width), F32),
            square, tall, tall,
            dma((2,)), dma((6, 6, 3)), dma((6, 6, 3)), dma((3, 3)), dma((3, 3)),
            dma((4,)), dma((4,)), dma, dma,
        ],
        compiler_params=pltpu.CompilerParams(
            collective_id=0, has_side_effects=True, vmem_limit_bytes=62 << 20
        ),
    )(view_one, view_two)
    return grad_one, grad_two, loss[0, 0]


def solution(mesh):
    return jax.shard_map(
        per_device,
        mesh=mesh,
        in_specs=(P("dp", None), P("dp", None)),
        out_specs=(P(("dp", "mp"), None), P(("dp", "mp"), None), P()),
        check_vma=False,
    )
```

time: 374 us -> 125 us (0.33); the launches traced: 368 us -> 124 us
  waiting for transfers between devices: 188 us -> 0 us
  Pallas kernels: 0 us -> 120 us
  matrix products: 79.2 us -> 0 us
  blocking collectives: 25.9 us -> 0 us
  other arithmetic: 21.1 us -> 0 us
  between operations: 18.3 us -> 0.64 us
  starting transfers between devices: 16.6 us -> 0 us
  local copies, waits for them, and re-layouts: 19.2 us -> 3.91 us
    psum x1 -> x0, waiting for transfers between devices: 125 us -> none  [per_device(): summed = lax.psum((gram_one, gram_two, gram_cross), 'dp')]
    pallas_call x0 -> x1, Pallas kernels: none -> 120 us  [per_device(): pl.pallas_call(body, name='cca', out_shape=(jax.ShapeDtypeStruct((rows //...]
    dot_general x20 -> x0, matrix products: 79.2 us -> none  [the longest x5 24 us: schulz_step(): return jnp.dot(full, target, preferred_element_type=jnp.float32)]
    all_gather x3 -> x0, waiting for transfers between devices: 44.6 us -> none  [side_by_side(): lax.all_gather(both, axis, axis=dim, tiled=True)]
    all_to_all x2 -> x0, waiting for transfers between devices: 18.2 us -> none  [copy_for_each(): lax.all_to_all(jnp.broadcast_to(x[None], (length, *x.shape)), axis, 0, 0,...]
    all_to_all x3 -> x0, blocking collectives: 17.4 us -> none  [copy_for_each(): lax.all_to_all(jnp.broadcast_to(x[None], (length, *x.shape)), axis, 0, 0,...]
    all_to_all x2 -> x0, starting transfers between devices: 16.1 us -> none  [copy_for_each(): lax.all_to_all(jnp.broadcast_to(x[None], (length, *x.shape)), axis, 0, 0,...]
    unnamed x3 -> x0, blocking collectives: 8.54 us -> none
  transfers between devices with their start and end apart: 6 -> 0, of which waited for: 6 -> 0; matrix products, arithmetic and copies ran while one was open for 1% -> 0% of each run, Pallas kernels for 0% -> 0%
where the time goes in v1:
time: 125 us; the launch traced here: 124 us
  Pallas kernels  120 us (96%)
  local copies, waits for them, and re-layouts  3.91 us (3%)
    pallas_call x1, Pallas kernels, per_device(): pl.pallas_call(body, name='cca', out_shape=(jax.ShapeDtypeStruct((rows //...  120 us
    unnamed x4, local copies, waits for them, and re-layouts  2.72 us

profile of v1, /device:TPU:1, one launch (start us, length us, event | category | flops | bytes accessed | tf_op | source)
XLA Modules:
  0.0 124.5 jit_solution(14947312199389339408)
XLA Ops:
  0.6 119.9 %cca.1 = (bf16[256,1024]{1,0:T(8,128)(2,1)}, bf16[256,1024]{1,0:T(8,128)(2,1)}, f32[8,128]{1,0:T(8,128)}) custom-call(bf16[512,1024]{1,0:T(8,128)(2,1)} %refs_0_.1, bf16[512,1024]{1,0:T(8,128)(2,1)} %refs_1_.1), custom_call_target="tpu_custom_call" | custom-call | tf_op jit(solution)/shard_map/cca/pallas_call | solution.py:339
  120.6 1.2 slice.3
  121.7 0.0 copy-start
  121.7 1.9 %copy.7 = bf16[256,1024]{1,0:T(8,128)(2,1)} copy(bf16[256,1024]{1,0:T(8,128)(2,1)} %get-tuple-element.12) | data formatting | bytes 1048576
  123.7 0.0 copy-done
  123.7 0.8 copy.8
Async XLA Ops:
  121.7 1.9 %copy-start = (bf16[256,1024]{1,0:T(8,128)(2,1)S(1)}, bf16[256,1024]{1,0:T(8,128)(2,1)}, u32[]{:S(2)}) copy-start(bf16[256,1024]{1,0:T(8,128)(2,1)} %get-tuple-element.13) | copy-start | bytes 1572868
